TPU v7x, 32 devices: a whole 2x2x4 slice. The times are simulated.
32 devices in a mesh: lat: 4 (over y, x), lon: 8 (over z, core).
Axes of the slice: x: 2, y: 2, z: 4, core: 2. Of those that a mesh axis runs over, the one named last changes fastest.
Arguments:
- latent_field: bfloat16 [640, 32, 64], P(None, 'lat', 'lon'), may hold values from -6 to 6
- spectral_filter: float32 [640, 32], P('lon'), may hold values from -5 to 5
- conv_weight: float32 [9, 640], replicated, may hold values from -2 to 2
- norm_gain: float32 [640], replicated, may hold values from 0.1 to 1.9
- weight_in: bfloat16 [640, 1280], replicated, may hold values from -0.25 to 0.25
- weight_out: bfloat16 [1280, 640], replicated, may hold values from -0.15625 to 0.15625
Outputs:
- updated: bfloat16 [640, 32, 64], P(None, 'lat', 'lon')
All inputs are finite; a program needn't handle non-finite values.
Results may differ from a plain program's by a relative error of at most 0.01.
Values may be sent and summed in bfloat16 or wider, within the bound.
A program may use at most 128 MiB of HBM per device.

v0:
```python
import math

import jax
import jax.numpy as jnp
from jax import lax
from jax.sharding import PartitionSpec as P

highest = lax.Precision.HIGHEST
epsilon_norm = 1e-06


def with_halo(cells, sides, width):
    for axis, dim in sides:
        count = lax.axis_size(axis)
        ends = count - 1
        head = lax.slice_in_dim(cells, 0, width, axis=dim)
        tail = lax.slice_in_dim(cells, cells.shape[dim] - width, cells.shape[dim], axis=dim)
        cells = jnp.concatenate(
            [
                lax.ppermute(tail, axis, [(i, (i + 1) % count) for i in range(ends)]),
                cells,
                lax.ppermute(head, axis, [((i + 1) % count, i) for i in range(ends)]),
            ],
            axis=dim,
        )
    return cells


def quadrature(lat_count):
    colatitude = (jnp.arange(lat_count, dtype=jnp.float32) + 0.5) * (math.pi / lat_count)
    return jnp.sin(colatitude) * (math.pi / lat_count)


def fourier_tables(lon_count, mode_count):
    wave_index = (
        jnp.arange(mode_count, dtype=jnp.int32)[:, None]
        * jnp.arange(lon_count, dtype=jnp.int32)[None, :]
    )
    phase_angle = (wave_index % lon_count).astype(jnp.float32) * (2.0 * math.pi / lon_count)
    cosine = jnp.cos(phase_angle)
    sine_table = jnp.sin(phase_angle)
    angle_step = 2.0 * math.pi / lon_count
    forward = jnp.concatenate([angle_step * cosine, -angle_step * sine_table], axis=0)
    weight = jnp.where(jnp.arange(mode_count, dtype=jnp.int32) == 0, 1.0, 2.0).astype(jnp.float32)[
        :, None
    ]
    inverse = jnp.concatenate([weight * cosine, -weight * sine_table], axis=0)
    return (forward, inverse)


def legendre_rows(order_ids, lat_count):
    colatitude = (jnp.arange(lat_count, dtype=jnp.float32) + 0.5) * (math.pi / lat_count)
    cosine = jnp.cos(colatitude)
    sine_col = jnp.sin(colatitude)
    order_f = order_ids.astype(jnp.float32)
    factor_index = jnp.arange(1, lat_count, dtype=jnp.float32)
    ratio_log = jnp.log((2.0 * factor_index - 1.0) / (2.0 * factor_index))
    included = (factor_index[None, :] <= order_f[:, None]).astype(jnp.float32)
    log_factor = jnp.sum(included * ratio_log[None, :], axis=1)
    start_log = 0.5 * jnp.log((2.0 * order_f + 1.0) / (4.0 * math.pi)) + 0.5 * log_factor
    start_log = start_log[:, None] + order_f[:, None] * jnp.log(sine_col)[None, :]
    blank_rows = jnp.zeros((order_ids.shape[0], lat_count), jnp.float32)
    order_col = order_f[:, None]

    def advance(state_carry, degree):
        before, current, scale_log = state_carry
        degree_f = degree.astype(jnp.float32)
        alpha_term = jnp.sqrt(
            (4.0 * degree_f * degree_f - 1.0)
            / jnp.maximum(degree_f * degree_f - order_col * order_col, 1.0)
        )
        beta_term = jnp.sqrt(
            jnp.maximum((degree_f - 1.0) ** 2 - order_col * order_col, 0.0)
            / jnp.maximum(4.0 * (degree_f - 1.0) ** 2 - 1.0, 1.0)
        )
        stepped = alpha_term * (cosine[None, :] * current - beta_term * before)
        at_start = order_ids[:, None] == degree
        past_start = order_ids[:, None] < degree
        fresh_value = jnp.where(at_start, 1.0, jnp.where(past_start, stepped, 0.0))
        fresh_log = jnp.where(at_start, start_log, scale_log)
        entry_value = fresh_value * jnp.exp(fresh_log)
        rescale = jnp.where(
            past_start | at_start, jnp.maximum(jnp.abs(fresh_value), jnp.abs(current)), 1.0
        )
        return (
            (current / rescale, fresh_value / rescale, fresh_log + jnp.log(rescale)),
            entry_value,
        )

    degrees = jnp.arange(lat_count, dtype=jnp.int32)
    unused, legendre = lax.scan(advance, (blank_rows, blank_rows, blank_rows), degrees, unroll=True)
    return legendre


def filter_modes(banded, legendre, filter_block, quad_weights):
    coefficients = jnp.einsum(
        "lmj,pmcj->pmcl", legendre, banded * quad_weights[None, None, None, :], precision=highest
    )
    coefficients = coefficients * filter_block[None, None, :, :]
    return jnp.einsum("lmj,pmcl->pmcj", legendre, coefficients, precision=highest)


def wrap_columns(extended):
    return jnp.concatenate([extended[:, :, -1:], extended, extended[:, :, :1]], axis=2)


def depthwise_core(extended, kernel, lat_rows, lon_cols):
    accumulated = jnp.zeros((extended.shape[0], lat_rows, lon_cols), jnp.float32)
    for row_shift in range(3):
        for col_shift in range(3):
            piece = extended[
                :, row_shift : row_shift + lat_rows, col_shift : col_shift + lon_cols
            ].astype(jnp.float32)
            accumulated = accumulated + kernel[3 * row_shift + col_shift][:, None, None] * piece
    return accumulated.astype(jnp.bfloat16)


def channel_mlp(summed_low, norm_gain, weight_in, weight_out):
    summed = summed_low.astype(jnp.float32)
    scale_inv = lax.rsqrt(jnp.mean(summed * summed, axis=0, keepdims=True) + epsilon_norm)
    normed = (summed * scale_inv * norm_gain[:, None]).astype(jnp.bfloat16)
    hidden = lax.dot_general(
        weight_in, normed, (((0,), (0,)), ((), ())), preferred_element_type=jnp.float32
    )
    hidden = jax.nn.gelu(hidden, approximate=False).astype(jnp.bfloat16)
    result = summed + lax.dot_general(
        weight_out, hidden, (((0,), (0,)), ((), ())), preferred_element_type=jnp.float32
    )
    return result.astype(jnp.bfloat16)


def add_three(first, second, third):
    total = first.astype(jnp.float32) + second.astype(jnp.float32) + third.astype(jnp.float32)
    return total.astype(jnp.bfloat16)


def on_device(latent_field, spectral_filter, conv_weight, norm_gain, weight_in, weight_out):
    channels, lat_rows, lon_cols = latent_field.shape
    sector_count = lax.axis_size("lon")
    lat_count = lat_rows * lax.axis_size("lat")
    lon_count = lon_cols * sector_count
    chan_block = channels // sector_count
    spread = lax.all_to_all(latent_field, "lon", split_axis=0, concat_axis=2, tiled=True)
    forward, inverse = fourier_tables(lon_count, lat_count)
    flattened = spread.astype(jnp.float32).reshape(chan_block * lat_rows, lon_count)
    spectrum = lax.dot_general(forward, flattened, (((1,), (1,)), ((), ())), precision=highest)
    spectrum = spectrum.reshape(2, lat_count, chan_block, lat_rows)
    banded = lax.all_to_all(spectrum, "lat", split_axis=1, concat_axis=3, tiled=True)
    order_ids = lax.axis_index("lat") * lat_rows + jnp.arange(lat_rows, dtype=jnp.int32)
    legendre = legendre_rows(order_ids, lat_count)
    synthesized = filter_modes(banded, legendre, spectral_filter, quadrature(lat_count))
    regathered = lax.all_to_all(synthesized, "lat", split_axis=3, concat_axis=1, tiled=True)
    regridded = lax.dot_general(
        regathered.reshape(2 * lat_count, chan_block * lat_rows),
        inverse,
        (((0,), (0,)), ((), ())),
        precision=highest,
    )
    spectral = regridded.reshape(chan_block, lat_rows, lon_count).astype(jnp.bfloat16)
    own_kernel = lax.dynamic_slice_in_dim(
        conv_weight, lax.axis_index("lon") * chan_block, chan_block, 1
    )
    rimmed = with_halo(spread, (("lat", 1),), 1)
    sector_mix = depthwise_core(wrap_columns(rimmed), own_kernel, lat_rows, lon_count)
    sector_sum = add_three(spread, spectral, sector_mix)
    summed = lax.all_to_all(sector_sum, "lon", split_axis=2, concat_axis=0, tiled=True)
    summed = summed.reshape(channels, lat_rows * lon_cols)
    result = channel_mlp(summed, norm_gain, weight_in, weight_out)
    return result.reshape(channels, lat_rows, lon_cols)


def solution(mesh):
    return jax.shard_map(
        on_device,
        mesh=mesh,
        in_specs=(P(None, "lat", "lon"), P("lon", None), P(), P(), P(), P()),
        out_specs=P(None, "lat", "lon"),
        check_vma=False,
    )
```

profile of v0, /device:TPU:0, one launch (start us, length us, event | category | flops | bytes accessed | tf_op | source)
XLA Modules:
  0.0 104.7 jit_solution(14487268147353196208)
XLA Ops:
  0.0 1.8 %copy.151 = bf16[640,8,8]{2,1,0:T(8,128)(2,1)S(1)} copy(bf16[640,8,8]{0,2,1:T(8,128)(2,1)} %param.6) | data formatting | bytes 163840 | tf_op args[0]
  1.8 2.0 %reshape.34176 = bf16[8,2,2560]{2,1,0:T(2,128)(2,1)} reshape(bf16[640,8,8]{2,1,0:T(8,128)(2,1)S(1)} %copy.151) | data formatting | bytes 163840
  3.8 6.4 %all-to-all-start = ((bf16[8,2,2560]{2,1,0:T(2,128)(2,1)}), bf16[8,2,2560]{2,1,0:T(2,128)(2,1)S(1)}, u32[]{:S(2)}, u32[]{:S(2)}) async-start(bf16[8,2,2560]{2,1,0:T(2,128)(2,1)} %reshape.34176), calls=%async_computation | async-start | bytes 163840 | tf_op jit(solution)/shard_map/all_to_all | solution.py:143
  24.9 1.2 %fusion.228 = (pred[8]{0:T(512)(128)(4,1)S(1)}, pred[8]{0:T(512)(128)(4,1)S(1)}, pred[8]{0:T(512)(128)(4,1)S(1)}, pred[8]{0:T(512)(128)(4,1)S(1)}, pred[8]{0:T(512)(128)(4,1)S(1)}, /*index=5*/pred[8]{0:T(512)(128)(4,1)S(1)}) fusion(s32[]{:T(128)} %bitcast.30, s32[]{:T(128)S(6)} %mul.5193, s32[]{:T(128)} %bitcast.29), kind=kLoop, calls=%fused_computation.521 | loop fusion | flops 56 | bytes 60 | tf_op jit(solution)/shard_map/eval_jaxpr/or | solution.py:83
  26.1 1.3 %fusion.236 = (pred[8]{0:T(512)(128)(4,1)S(1)}, pred[8]{0:T(512)(128)(4,1)S(1)}, pred[8]{0:T(512)(128)(4,1)S(1)}, pred[8]{0:T(512)(128)(4,1)S(1)}, pred[8]{0:T(512)(128)(4,1)S(1)}, /*index=5*/pred[8]{0:T(512)(128)(4,1)S(1)}) fusion(s32[]{:T(128)} %bitcast.28, s32[]{:T(128)S(6)} %mul.5193, s32[]{:T(128)} %bitcast.27), kind=kLoop, calls=%fused_computation.525 | loop fusion | flops 56 | bytes 60 | tf_op jit(solution)/shard_map/eval_jaxpr/or | solution.py:83
  27.4 1.3 %fusion.244 = (pred[8]{0:T(512)(128)(4,1)S(1)}, pred[8]{0:T(512)(128)(4,1)S(1)}, pred[8]{0:T(512)(128)(4,1)S(1)}, pred[8]{0:T(512)(128)(4,1)S(1)}, pred[8]{0:T(512)(128)(4,1)S(1)}, /*index=5*/pred[8]{0:T(512)(128)(4,1)S(1)}) fusion(s32[]{:T(128)} %bitcast.26, s32[]{:T(128)S(6)} %mul.5193, s32[]{:T(128)} %bitcast.25), kind=kLoop, calls=%fused_computation.529 | loop fusion | flops 56 | bytes 60 | tf_op jit(solution)/shard_map/eval_jaxpr/or | solution.py:83
  28.7 1.3 %fusion.221 = (pred[8]{0:T(512)(128)(4,1)S(1)}, pred[8]{0:T(512)(128)(4,1)S(1)}, pred[8]{0:T(512)(128)(4,1)S(1)}, pred[8]{0:T(512)(128)(4,1)S(1)}, pred[8]{0:T(512)(128)(4,1)S(1)}, /*index=5*/pred[8]{0:T(512)(128)(4,1)S(1)}) fusion(s32[]{:T(128)} %bitcast.32, s32[]{:T(128)S(6)} %mul.5193, s32[]{:T(128)} %bitcast.31), kind=kLoop, calls=%fused_computation.518 | loop fusion | flops 56 | bytes 60 | tf_op jit(solution)/shard_map/eval_jaxpr/or | solution.py:83
  30.0 1.4 %fusion.252 = (pred[8]{0:T(512)(128)(4,1)S(1)}, pred[8]{0:T(512)(128)(4,1)S(1)}, pred[8]{0:T(512)(128)(4,1)S(1)}, pred[8]{0:T(512)(128)(4,1)S(1)}, pred[8]{0:T(512)(128)(4,1)S(1)}, /*index=5*/pred[8]{0:T(512)(128)(4,1)S(1)}) fusion(s32[]{:T(128)} %bitcast.24, s32[]{:T(128)S(6)} %mul.5193, s32[]{:T(128)} %bitcast.23), kind=kLoop, calls=%fused_computation.533 | loop fusion | flops 56 | bytes 60 | tf_op jit(solution)/shard_map/eval_jaxpr/or | solution.py:83
  31.4 1.2 %fusion.260 = (pred[8]{0:T(512)(128)(4,1)S(1)}, pred[8]{0:T(512)(128)(4,1)S(1)}, pred[8]{0:T(512)(128)(4,1)S(1)}, pred[8]{0:T(512)(128)(4,1)S(1)}, pred[8]{0:T(512)(128)(4,1)S(1)}, /*index=5*/pred[8]{0:T(512)(128)(4,1)S(1)}) fusion(s32[]{:T(128)} %bitcast.22, s32[]{:T(128)S(6)} %mul.5193, s32[]{:T(128)} %bitcast.21), kind=kLoop, calls=%fused_computation.537 | loop fusion | flops 56 | bytes 60 | tf_op jit(solution)/shard_map/eval_jaxpr/or | solution.py:83
  32.5 1.3 %fusion.268 = (pred[8]{0:T(512)(128)(4,1)S(1)}, pred[8]{0:T(512)(128)(4,1)S(1)}, pred[8]{0:T(512)(128)(4,1)S(1)}, pred[8]{0:T(512)(128)(4,1)S(1)}, pred[8]{0:T(512)(128)(4,1)S(1)}, /*index=5*/pred[8]{0:T(512)(128)(4,1)S(1)}) fusion(s32[]{:T(128)} %bitcast.20, s32[]{:T(128)S(6)} %mul.5193, s32[]{:T(128)} %bitcast.19), kind=kLoop, calls=%fused_computation.541 | loop fusion | flops 56 | bytes 60 | tf_op jit(solution)/shard_map/eval_jaxpr/or | solution.py:83
  33.9 1.1 %fusion.276 = (pred[8]{0:T(512)(128)(4,1)S(1)}, pred[8]{0:T(512)(128)(4,1)S(1)}, pred[8]{0:T(512)(128)(4,1)S(1)}, pred[8]{0:T(512)(128)(4,1)S(1)}, pred[8]{0:T(512)(128)(4,1)S(1)}, /*index=5*/pred[8]{0:T(512)(128)(4,1)S(1)}) fusion(s32[]{:T(128)} %bitcast.18, s32[]{:T(128)S(6)} %mul.5193, s32[]{:T(128)} %bitcast.17), kind=kLoop, calls=%fused_computation.545 | loop fusion | flops 56 | bytes 60 | tf_op jit(solution)/shard_map/eval_jaxpr/or | solution.py:83
  35.0 1.4 %fusion.284 = (pred[8]{0:T(512)(128)(4,1)S(1)}, pred[8]{0:T(512)(128)(4,1)S(1)}, pred[8]{0:T(512)(128)(4,1)S(1)}, pred[8]{0:T(512)(128)(4,1)S(1)}, pred[8]{0:T(512)(128)(4,1)S(1)}, /*index=5*/pred[8]{0:T(512)(128)(4,1)S(1)}) fusion(s32[]{:T(128)} %bitcast.16, s32[]{:T(128)S(6)} %mul.5193, s32[]{:T(128)} %bitcast.15), kind=kLoop, calls=%fused_computation.549 | loop fusion | flops 56 | bytes 60 | tf_op jit(solution)/shard_map/eval_jaxpr/or | solution.py:83
  36.4 1.3 %fusion.292 = (pred[8]{0:T(512)(128)(4,1)S(1)}, pred[8]{0:T(512)(128)(4,1)S(1)}, pred[8]{0:T(512)(128)(4,1)S(1)}, pred[8]{0:T(512)(128)(4,1)S(1)}, pred[8]{0:T(512)(128)(4,1)S(1)}, /*index=5*/pred[8]{0:T(512)(128)(4,1)S(1)}) fusion(s32[]{:T(128)} %bitcast.14, s32[]{:T(128)S(6)} %mul.5193, s32[]{:T(128)} %bitcast.13), kind=kLoop, calls=%fused_computation.553 | loop fusion | flops 56 | bytes 60 | tf_op jit(solution)/shard_map/eval_jaxpr/or | solution.py:83
  45.1 1.3 %fusion.191 = (pred[8]{0:T(512)(128)(4,1)S(1)}, pred[8]{0:T(512)(128)(4,1)S(1)}, pred[8]{0:T(512)(128)(4,1)S(1)}, pred[8]{0:T(512)(128)(4,1)S(1)}, pred[8]{0:T(512)(128)(4,1)S(1)}, /*index=5*/pred[8]{0:T(512)(128)(4,1)S(1)}) fusion(s32[]{:T(128)} %bitcast.59, s32[]{:T(128)S(6)} %mul.5193, s32[]{:T(128)} %bitcast.57), kind=kLoop, calls=%fused_computation.508 | loop fusion | flops 56 | bytes 60 | tf_op jit(solution)/shard_map/eval_jaxpr/or | solution.py:83
  46.4 1.2 %fusion.197 = (pred[8]{0:T(512)(128)(4,1)S(1)}, pred[8]{0:T(512)(128)(4,1)S(1)}, pred[8]{0:T(512)(128)(4,1)S(1)}, pred[8]{0:T(512)(128)(4,1)S(1)}, pred[8]{0:T(512)(128)(4,1)S(1)}, /*index=5*/pred[8]{0:T(512)(128)(4,1)S(1)}) fusion(s32[]{:T(128)} %bitcast.54, s32[]{:T(128)S(6)} %mul.5193, s32[]{:T(128)} %bitcast.51), kind=kLoop, calls=%fused_computation.510 | loop fusion | flops 56 | bytes 60 | tf_op jit(solution)/shard_map/eval_jaxpr/or | solution.py:83
  47.6 1.3 %fusion.203 = (pred[8]{0:T(512)(128)(4,1)S(1)}, pred[8]{0:T(512)(128)(4,1)S(1)}, pred[8]{0:T(512)(128)(4,1)S(1)}, pred[8]{0:T(512)(128)(4,1)S(1)}, pred[8]{0:T(512)(128)(4,1)S(1)}, /*index=5*/pred[8]{0:T(512)(128)(4,1)S(1)}) fusion(s32[]{:T(128)} %bitcast.48, s32[]{:T(128)S(6)} %mul.5193, s32[]{:T(128)} %bitcast.45), kind=kLoop, calls=%fused_computation.512 | loop fusion | flops 56 | bytes 60 | tf_op jit(solution)/shard_map/eval_jaxpr/or | solution.py:83
  48.9 1.1 %fusion.209 = (pred[8]{0:T(512)(128)(4,1)S(1)}, pred[8]{0:T(512)(128)(4,1)S(1)}, pred[8]{0:T(512)(128)(4,1)S(1)}, pred[8]{0:T(512)(128)(4,1)S(1)}, pred[8]{0:T(512)(128)(4,1)S(1)}, /*index=5*/pred[8]{0:T(512)(128)(4,1)S(1)}) fusion(s32[]{:T(128)} %bitcast.42, s32[]{:T(128)S(6)} %mul.5193, s32[]{:T(128)} %bitcast.39), kind=kLoop, calls=%fused_computation.514 | loop fusion | flops 56 | bytes 60 | tf_op jit(solution)/shard_map/eval_jaxpr/or | solution.py:83
  50.0 1.2 %fusion.215 = (pred[8]{0:T(512)(128)(4,1)S(1)}, pred[8]{0:T(512)(128)(4,1)S(1)}, pred[8]{0:T(512)(128)(4,1)S(1)}, pred[8]{0:T(512)(128)(4,1)S(1)}, pred[8]{0:T(512)(128)(4,1)S(1)}, /*index=5*/pred[8]{0:T(512)(128)(4,1)S(1)}) fusion(s32[]{:T(128)} %bitcast.36, s32[]{:T(128)S(6)} %mul.5193, s32[]{:T(128)} %bitcast.33), kind=kLoop, calls=%fused_computation.516 | loop fusion | flops 56 | bytes 60 | tf_op jit(solution)/shard_map/eval_jaxpr/or | solution.py:83
  58.3 1.5 %reshape.34177 = bf16[640,8,8]{2,1,0:T(8,128)(2,1)S(1)} reshape(bf16[8,2,2560]{2,1,0:T(2,128)(2,1)S(1)} %all-to-all-done) | data formatting | bytes 163840
  59.8 0.9 copy.152
  61.8 3.7 %all-to-all-start.1 = ((f32[2,32,80,8]{2,3,0,1:T(8,128)}), f32[2,32,80,8]{2,3,0,1:T(8,128)S(1)}, u32[]{:S(2)}, u32[]{:S(2)}) async-start(f32[2,32,80,8]{2,3,0,1:T(8,128)} %copy.154), calls=%async_computation.1 | async-start | bytes 524288 | tf_op jit(solution)/shard_map/all_to_all | solution.py:148
  65.6 3.9 %collective-permute-start = (bf16[80,1,64]{0,2,1:T(8,128)(2,1)S(1)}, bf16[80,1,64]{0,2,1:T(8,128)(2,1)S(1)}, u32[]{:S(2)}, u32[]{:S(2)}) collective-permute-start(bf16[80,1,64]{0,2,1:T(8,128)(2,1)S(1)} %get-tuple-element.211), channel_id=1, source_target_pairs={{0,8},{8,16},{16,24},{1,9},{9,17},{17,25},{2,10},{10,18},{18,26},{... | collective-permute-start | bytes 30728 | tf_op jit(solution)/shard_map/ppermute | solution.py:20
  69.5 1.3 %collective-permute-start.1 = (bf16[80,1,64]{0,2,1:T(8,128)(2,1)S(1)}, bf16[80,1,64]{0,2,1:T(8,128)(2,1)S(1)}, u32[]{:S(2)}, u32[]{:S(2)}) collective-permute-start(bf16[80,1,64]{0,2,1:T(8,128)(2,1)S(1)} %get-tuple-element.212), channel_id=1, source_target_pairs={{8,0},{16,8},{24,16},{9,1},{17,9},{25,17},{10,2},{18,10},{26,18},{... | collective-permute-start | bytes 30728 | tf_op jit(solution)/shard_map/ppermute | solution.py:22
  72.5 0.9 copy.169
  73.4 4.0 %all-to-all-start.2 = ((f32[2,8,80,32]{2,0,1,3:T(2,128)}), f32[2,8,80,32]{2,0,1,3:T(2,128)S(1)}, u32[]{:S(2)}, u32[]{:S(2)}) async-start(f32[2,8,80,32]{2,0,1,3:T(2,128)} %copy.169), calls=%async_computation.2 | async-start | bytes 524288 | tf_op jit(solution)/shard_map/all_to_all | solution.py:152
  77.4 1.1 %dynamic-slice_bitcast_fusion.8 = (f32[80]{0:T(128)S(1)}, f32[80]{0:T(128)S(1)}, f32[80]{0:T(128)S(1)}, f32[80]{0:T(128)S(1)}, f32[80]{0:T(128)S(1)}, /*index=5*...) fusion(f32[9,640]{1,0:T(8,128)} %param.8, s32[]{:T(128)S(6)} %select_n.4652, s32[]{:T(128)S(6)} %add.2017, ...), kind=kLoop, calls=%fused_computation.336 | loop fusion | bytes 5796 | tf_op jit(solution)/shard_map/mul | solution.py:114
  78.6 4.4 %all-to-all-done.2 = f32[2,8,80,32]{2,0,1,3:T(2,128)S(1)} async-done(((f32[2,8,80,32]{2,0,1,3:T(2,128)}), f32[2,8,80,32]{2,0,1,3:T(2,128)S(1)}, u32[]{:S(2)}, u32[]{:S(2)}) %all-to-all-start.2) | async-done | bytes 163872 | tf_op jit(solution)/shard_map/all_to_all | solution.py:152
  83.0 2.0 %copy.170 = f32[2,8,80,4,8]{4,2,1,3,0:T(8,128)} copy(f32[2,8,80,4,8]{2,0,1,4,3:T(2,128)S(1)} %bitcast.273) | data formatting | bytes 327680 | tf_op jit(solution)/shard_map/all_to_all | solution.py:152
  84.9 3.0 %reshape.34167 = f32[64,640]{1,0:T(8,128)S(1)} reshape(f32[2,4,8,80,8]{4,3,2,1,0:T(8,128)} %bitcast.265) | data formatting | bytes 327680 | tf_op jit(solution)/shard_map/reshape | solution.py:154
  88.1 1.1 %fusion.4 = bf16[80,8,64]{0,2,1:T(8,128)(2,1)S(1)} fusion(bf16[80,8,64]{0,2,1:T(8,128)(2,1)S(1)} %bitcast.269, f32[80,8,64]{2,1,0:T(8,128)S(1)} %bitcast.275, bf16[80,10,65]{0,2,1:T(8,128)(2,1)S(1)} %get-tuple-element.210, bf16[80,1,64]{0,2,1:T(8,128)(2,1)S(1)} %collective-permute-done.1, bf16[80,10,65]{0,2,1:T(8,128)(2,1)S(1)} %get-tuple-element.209, ...), kind=kOutput, calls=%fused_computation.7 | convolution fusion | flops 32894976 | bytes 858944 | tf_op jit(solution)/shard_map/dot_general | solution.py:153
  89.3 11.5 %all_to_all.60 = bf16[80,8,64]{0,1,2:T(8,128)(2,1)S(1)} all-to-all(bf16[80,8,64]{0,1,2:T(8,128)(2,1)S(1)} %copy.173), channel_id=1, replica_groups=mesh['lat'=4,'lon'=8] {'lon'}, dimensions={2} | all-to-all | bytes 163840 | tf_op jit(solution)/shard_map/all_to_all | solution.py:166
  101.4 3.4 %fusion.7 = bf16[640,8,8]{0,2,1:T(8,128)(2,1)} fusion(f32[640,64]{0,1:T(8,128)S(1)} %reshape.34169, bf16[1280,640]{1,0:T(8,128)(2,1)S(1)} %copy-done, bf16[640,1280]{1,0:T(8,128)(2,1)} %param.10, f32[640]{0:T(1024)S(1)} %copy-done.2, f32[64]{0:T(128)S(1)} %rsqrt.12), kind=kOutput, calls=%fused_computation.11 | convolution fusion | flops 215244800 | bytes 3525376 | tf_op jit(solution)/shard_map/dot_general | solution.py:126
  (120 shorter events, 12.0 us)
Async XLA Ops:
  0.0 101.4 %copy-start = (bf16[1280,640]{1,0:T(8,128)(2,1)S(1)}, bf16[1280,640]{1,0:T(8,128)(2,1)}, u32[]{:S(2)}) copy-start(bf16[1280,640]{1,0:T(8,128)(2,1)} %param.11) | copy-start | bytes 4915204
  3.8 54.4 %all-to-all-start = ((bf16[8,2,2560]{2,1,0:T(2,128)(2,1)}), bf16[8,2,2560]{2,1,0:T(2,128)(2,1)S(1)}, u32[]{:S(2)}, u32[]{:S(2)}) async-start(bf16[8,2,2560]{2,1,0:T(2,128)(2,1)} %reshape.34176), calls=%async_computation | async-start | bytes 163840 | tf_op jit(solution)/shard_map/all_to_all | solution.py:143
  59.8 11.8 %copy-start.1 = (f32[80,32]{0,1:T(8,128)S(1)}, f32[80,32]{0,1:T(8,128)}, u32[]{:S(2)}) copy-start(f32[80,32]{0,1:T(8,128)} %param.7) | copy-start | bytes 30724
  61.8 9.7 %all-to-all-start.1 = ((f32[2,32,80,8]{2,3,0,1:T(8,128)}), f32[2,32,80,8]{2,3,0,1:T(8,128)S(1)}, u32[]{:S(2)}, u32[]{:S(2)}) async-start(f32[2,32,80,8]{2,3,0,1:T(8,128)} %copy.154), calls=%async_computation.1 | async-start | bytes 524288 | tf_op jit(solution)/shard_map/all_to_all | solution.py:148
  65.6 12.9 %collective-permute-start = (bf16[80,1,64]{0,2,1:T(8,128)(2,1)S(1)}, bf16[80,1,64]{0,2,1:T(8,128)(2,1)S(1)}, u32[]{:S(2)}, u32[]{:S(2)}) collective-permute-start(bf16[80,1,64]{0,2,1:T(8,128)(2,1)S(1)} %get-tuple-element.211), channel_id=1, source_target_pairs={{0,8},{8,16},{16,24},{1,9},{9,17},{17,25},{2,10},{10,18},{18,26},{... | collective-permute-start | bytes 30728 | tf_op jit(solution)/shard_map/ppermute | solution.py:20
  69.5 9.0 %collective-permute-start.1 = (bf16[80,1,64]{0,2,1:T(8,128)(2,1)S(1)}, bf16[80,1,64]{0,2,1:T(8,128)(2,1)S(1)}, u32[]{:S(2)}, u32[]{:S(2)}) collective-permute-start(bf16[80,1,64]{0,2,1:T(8,128)(2,1)S(1)} %get-tuple-element.212), channel_id=1, source_target_pairs={{8,0},{16,8},{24,16},{9,1},{17,9},{25,17},{10,2},{18,10},{26,18},{... | collective-permute-start | bytes 30728 | tf_op jit(solution)/shard_map/ppermute | solution.py:22
  73.4 9.6 %all-to-all-start.2 = ((f32[2,8,80,32]{2,0,1,3:T(2,128)}), f32[2,8,80,32]{2,0,1,3:T(2,128)S(1)}, u32[]{:S(2)}, u32[]{:S(2)}) async-start(f32[2,8,80,32]{2,0,1,3:T(2,128)} %copy.169), calls=%async_computation.2 | async-start | bytes 524288 | tf_op jit(solution)/shard_map/all_to_all | solution.py:152
  88.1 13.3 %copy-start.2 = (f32[640]{0:T(1024)S(1)}, f32[640]{0:T(1024)}, u32[]{:S(2)}) copy-start(f32[640]{0:T(1024)} %param.9) | copy-start | bytes 7684
where the time goes:
time: 106 us; the launch traced here: 105 us
  other arithmetic  25.6 us (24%)
  between operations  21.1 us (20%)
  starting transfers between devices  19.3 us (18%)
  local copies, waits for them, and re-layouts  16.4 us (15%)
  blocking collectives  11.5 us (11%)
  matrix products  5.57 us (5%)
  waiting for transfers between devices  5.18 us (5%)
    or x16, other arithmetic, advance(): past_start | at_start  19.3 us
    all_to_all x1, blocking collectives, on_device(): lax.all_to_all(sector_sum, 'lon', split_axis=2, concat_axis=0, tiled=True)  11.5 us
    all_to_all x1, starting transfers between devices, on_device(): lax.all_to_all(latent_field, 'lon', split_axis=0, concat_axis=2, tiled=True)  6.35 us
    unnamed x9, local copies, waits for them, and re-layouts  5.37 us
    all_to_all x1, waiting for transfers between devices, on_device(): lax.all_to_all(synthesized, 'lat', split_axis=3, concat_axis=1, tiled=True)  4.37 us
    all_to_all x1, starting transfers between devices, on_device(): lax.all_to_all(synthesized, 'lat', split_axis=3, concat_axis=1, tiled=True)  4.03 us
    ppermute x1, starting transfers between devices, with_halo(): lax.ppermute(tail, axis, [(i, (i + 1) % count) for i in range(ends)])  3.92 us
    all_to_all x1, starting transfers between devices, on_device(): lax.all_to_all(spectrum, 'lat', split_axis=1, concat_axis=3, tiled=True)  3.71 us
  transfers between devices with their start and end apart: 5, of which 2 were waited for; matrix products, arithmetic and copies ran while one was open for 29% of the time, Pallas kernels for 0%

commit v1 on v0

--- a/solution.py
+++ b/solution.py
@@ -1,7 +1,9 @@
+import functools
 import math
 
 import jax
 import jax.numpy as jnp
+import numpy as np
 from jax import lax
 from jax.sharding import PartitionSpec as P
 
@@ -88,7 +90,7 @@
         )
 
     degrees = jnp.arange(lat_count, dtype=jnp.int32)
-    unused, legendre = lax.scan(advance, (blank_rows, blank_rows, blank_rows), degrees, unroll=True)
+    unused, legendre = lax.scan(advance, (blank_rows, blank_rows, blank_rows), degrees)
     return legendre
 
 
@@ -169,9 +171,103 @@
     return result.reshape(channels, lat_rows, lon_cols)
 
 
+def transform_factors(lat_count, lon_count):
+    theta = (np.arange(lat_count) + 0.5) * (math.pi / lat_count)
+    x, s = np.cos(theta), np.sin(theta)
+    quad = s * (math.pi / lat_count)
+    phi = 2.0 * math.pi * np.arange(lon_count) / lon_count
+    legendre, cosine, sine, degree, order = [], [], [], [], []
+    for m in range(lat_count):
+        k = np.arange(1, m + 1)
+        log_start = 0.5 * (np.log((2 * m + 1) / (4 * math.pi)) + np.sum(np.log((2 * k - 1) / (2 * k))))
+        before, current = np.zeros(lat_count), np.exp(log_start + m * np.log(s))
+        for l in range(m, lat_count):
+            if l > m:
+                a = math.sqrt((4.0 * l * l - 1) / (l * l - m * m))
+                b = math.sqrt(((l - 1.0) ** 2 - m * m) / (4.0 * (l - 1) ** 2 - 1))
+                before, current = current, a * (x * current - b * before)
+            legendre.append(current)
+            cosine.append(np.cos(m * phi))
+            sine.append(-np.sin(m * phi))
+            degree.append(l)
+            order.append(m)
+    legendre = np.stack(legendre, 1)
+    cosine, sine = np.stack(cosine, 1), np.stack(sine, 1)
+    degree, order = np.array(degree), np.array(order)
+    legendre = np.concatenate([legendre, legendre], 1)
+    fourier = np.concatenate([cosine, sine], 1)
+    weight = np.where(np.concatenate([order, order]) == 0, 1.0, 2.0)
+    select = (np.arange(lat_count)[:, None] == np.concatenate([degree, degree])[None, :])
+    forward = fourier * (2.0 * math.pi / lon_count)
+    f32 = np.float32
+    return (
+        (legendre * quad[:, None]).astype(f32),
+        forward.astype(f32),
+        legendre.astype(f32),
+        (fourier * weight).astype(f32),
+        select.astype(f32),
+    )
+
+
+def full_table(rows, columns, lat_devices, lon_devices):
+    width = rows.shape[1]
+    rows = jnp.asarray(rows).reshape(lat_devices, 1, -1, 1, width)
+    columns = jnp.asarray(columns).reshape(1, lon_devices, 1, -1, width)
+    return (rows * columns).astype(jnp.bfloat16).reshape(-1, width)
+
+
+def whole_sphere(lat_devices, lon_devices, latent_field, spectral_filter, conv_weight, norm_gain, weight_in, weight_out):
+    channels, lat_rows, lon_cols = latent_field.shape
+    devices = lat_devices * lon_devices
+    lat_count, lon_count = lat_rows * lat_devices, lon_cols * lon_devices
+    points = lat_rows * lon_cols
+    own = channels // devices
+    me_lat, me_lon = lax.axis_index("lat"), lax.axis_index("lon")
+    start = (me_lat * lon_devices + me_lon) * own
+    axes = ("lat", "lon")
+    mine = lax.all_to_all(
+        latent_field.reshape(devices, own, points), axes, split_axis=0, concat_axis=0, tiled=True
+    )
+    rows_f, cols_f, rows_i, cols_i, select = transform_factors(lat_count, lon_count)
+    analysis = full_table(rows_f, cols_f, lat_devices, lon_devices)
+    synthesis = full_table(rows_i, cols_i, lat_devices, lon_devices)
+    filters = lax.all_gather(spectral_filter, "lon", axis=0, tiled=True)
+    own_filter = lax.dynamic_slice_in_dim(filters, start, own, 0)
+    gain = lax.dot_general(
+        own_filter, jnp.asarray(select), (((1,), (0,)), ((), ())), precision=highest
+    )
+    flat = jnp.transpose(mine, (1, 0, 2)).reshape(own, devices * points)
+    coefficients = lax.dot_general(
+        flat, analysis, (((1,), (0,)), ((), ())), preferred_element_type=jnp.float32
+    )
+    coefficients = (coefficients * gain).astype(jnp.bfloat16)
+    spectral = lax.dot_general(
+        coefficients, synthesis, (((1,), (1,)), ((), ())), preferred_element_type=jnp.float32
+    ).astype(jnp.bfloat16)
+    spectral = spectral.reshape(own, lat_devices, lon_devices, lat_rows, lon_cols)
+    own_kernel = lax.dynamic_slice_in_dim(conv_weight, start, own, 1)
+    grid = flat.reshape(own, lat_devices, lon_devices, lat_rows, lon_cols)
+    grid = jnp.transpose(grid, (0, 1, 3, 2, 4)).reshape(own, lat_count, lon_count)
+    spectral = jnp.transpose(spectral, (0, 1, 3, 2, 4)).reshape(own, lat_count, lon_count)
+    rimmed = jnp.pad(grid, ((0, 0), (1, 1), (0, 0)))
+    mix = depthwise_core(wrap_columns(rimmed), own_kernel, lat_count, lon_count)
+    total = add_three(grid, spectral, mix)
+    total = total.reshape(own, lat_devices, lat_rows, lon_devices, lon_cols)
+    total = jnp.transpose(total, (1, 3, 0, 2, 4)).reshape(devices, own, points)
+    summed = lax.all_to_all(total, axes, split_axis=0, concat_axis=0, tiled=True)
+    result = channel_mlp(summed.reshape(channels, points), norm_gain, weight_in, weight_out)
+    return result.reshape(channels, lat_rows, lon_cols)
+
+
+def whole_or_banded(lat_devices, lon_devices, *arguments):
+    if arguments[0].shape[0] % (lat_devices * lon_devices) == 0:
+        return whole_sphere(lat_devices, lon_devices, *arguments)
+    return on_device(*arguments)
+
+
 def solution(mesh):
     return jax.shard_map(
-        on_device,
+        functools.partial(whole_or_banded, mesh.shape["lat"], mesh.shape["lon"]),
         mesh=mesh,
         in_specs=(P(None, "lat", "lon"), P("lon", None), P(), P(), P(), P()),
         out_specs=P(None, "lat", "lon"),

time: 106 us -> 63.8 us (0.60)
  between operations: 21.1 us -> 0.17 us
  other arithmetic: 25.6 us -> 9.14 us
  blocking collectives: 11.5 us -> 27.3 us
  starting transfers between devices: 19.3 us -> 7.33 us
  local copies, waits for them, and re-layouts: 16.4 us -> 11 us
  waiting for transfers between devices: 5.18 us -> 0.01 us
  matrix products: 5.57 us -> 8.54 us
    or x16 -> x0, other arithmetic: 19.3 us -> none  [advance(): past_start | at_start]
    all_gather x0 -> x1, blocking collectives: none -> 14.4 us  [whole_sphere(): filters = lax.all_gather(spectral_filter, 'lon', axis=0, tiled=True)]
    convert_element_type x1 -> x3, other arithmetic: 0.01 us -> 9.01 us  [the longest x2 7.86 us: full_table(): return (rows * columns).astype(jnp.bfloat16).reshape(-1, width)]
    all_to_all x3 -> x1, starting transfers between devices: 14.1 us -> 7.33 us  [whole_sphere(): lax.all_to_all(latent_field.reshape(devices, own, points), axes, split_ax...]
    ppermute x2 -> x0, starting transfers between devices: 5.21 us -> none  [the longest x1 3.92 us: with_halo(): lax.ppermute(tail, axis, [(i, (i + 1) % count) for i in range(ends)])]
    all_to_all x3 -> x1, waiting for transfers between devices: 5.18 us -> 0.01 us  [whole_sphere(): lax.all_to_all(latent_field.reshape(devices, own, points), axes, split_ax...]
    unnamed x9 -> x19, local copies, waits for them, and re-layouts: 5.37 us -> 1.52 us
    convert_element_type x0 -> x3, local copies, waits for them, and re-layouts: none -> 3.16 us  [add_three(): second.astype(jnp.float32)]
  transfers between devices with their start and end apart: 5 -> 1, of which waited for: 2 -> 0; matrix products, arithmetic and copies ran while one was open for 29% -> 14% of each run, Pallas kernels for 0% -> 0%
where the time goes in v1:
time: 63.8 us; the launch traced here: 63.5 us
  blocking collectives  27.3 us (43%)
  local copies, waits for them, and re-layouts  11 us (17%)
  other arithmetic  9.14 us (14%)
  matrix products  8.54 us (13%)
  starting transfers between devices  7.33 us (11%)
    all_gather x1, blocking collectives, whole_sphere(): filters = lax.all_gather(spectral_filter, 'lon', axis=0, tiled=True)  14.4 us
    all_to_all x1, blocking collectives, whole_sphere(): lax.all_to_all(total, axes, split_axis=0, concat_axis=0, tiled=True)  12.9 us
    convert_element_type x2, other arithmetic, full_table(): return (rows * columns).astype(jnp.bfloat16).reshape(-1, width)  7.86 us
    all_to_all x1, starting transfers between devices, whole_sphere(): lax.all_to_all(latent_field.reshape(devices, own, points), axes, split_ax...  7.33 us
    dot_general x1, matrix products, channel_mlp(): lax.dot_general(weight_out, hidden, (((0,), (0,)), ((), ())), preferred_e...  3.62 us
    dot_general x1, matrix products, whole_sphere(): lax.dot_general(flat, analysis, (((1,), (0,)), ((), ())), preferred_eleme...  3.21 us
    convert_element_type x3, local copies, waits for them, and re-layouts, add_three(): second.astype(jnp.float32)  3.16 us
    reshape x2, local copies, waits for them, and re-layouts, whole_sphere(): latent_field.reshape(devices, own, points)  2.95 us
  transfers between devices with their start and end apart: 1, of which 0 were waited for; matrix products, arithmetic and copies ran while one was open for 14% of the time, Pallas kernels for 0%

profile of v1, /device:TPU:0, one launch (start us, length us, event | category | flops | bytes accessed | tf_op | source)
XLA Modules:
  0.0 63.5 jit_solution(10295145786277437358)
XLA Ops:
  0.0 2.3 %reshape.71 = bf16[32,20,64]{1,0,2:T(8,128)(2,1)S(1)} reshape(bf16[640,8,8]{0,2,1:T(8,128)(2,1)} %param.11) | data formatting | bytes 163840 | tf_op jit(solution)/shard_map/reshape | solution.py:229
  2.3 0.7 %copy.75 = bf16[32,20,64]{2,1,0:T(8,128)(2,1)S(1)} copy(bf16[32,20,64]{1,0,2:T(8,128)(2,1)S(1)} %reshape.71) | data formatting | bytes 163840 | tf_op jit(solution)/shard_map/reshape | solution.py:229
  3.0 0.8 %reshape.82 = bf16[32,2,640]{2,1,0:T(2,128)(2,1)} reshape(bf16[32,20,64]{2,1,0:T(8,128)(2,1)S(1)} %copy.75) | data formatting | bytes 163840
  3.8 7.3 %all-to-all-start = ((bf16[32,2,640]{2,1,0:T(2,128)(2,1)}), bf16[32,2,640]{2,1,0:T(2,128)(2,1)S(1)}, u32[]{:S(2)}, u32[]{:S(2)}) async-start(bf16[32,2,640]{2,1,0:T(2,128)(2,1)} %reshape.82), calls=%async_computation | async-start | bytes 163840 | tf_op jit(solution)/shard_map/all_to_all | solution.py:228
  11.1 4.4 %multiply_convert_fusion.1 = bf16[4,8,8,8,1056]{4,3,2,1,0:T(8,128)(2,1)} fusion(f32[8,8,1056]{2,1,0:T(8,128)} %constant.102, f32[4,8,1056]{2,1,0:T(8,128)} %constant.101), kind=kLoop, calls=%fused_computation.1 | loop fusion | flops 4325376 | bytes 4730880 | tf_op jit(solution)/shard_map/convert_element_type | solution.py:216
  15.6 3.4 %multiply_convert_fusion = bf16[4,8,8,8,1056]{4,3,2,1,0:T(8,128)(2,1)} fusion(f32[8,8,1056]{2,1,0:T(8,128)S(1)} %copy-done.2, f32[4,8,1056]{2,1,0:T(8,128)S(1)} %copy-done.3), kind=kLoop, calls=%fused_computation | loop fusion | flops 4325376 | bytes 4730880 | tf_op jit(solution)/shard_map/convert_element_type | solution.py:216
  19.0 14.4 %all-gather = f32[8,80,32]{1,2,0:T(8,128)S(1)} all-gather(f32[1,80,32]{1,2,0:T(8,128)S(1)} %bitcast.133), channel_id=1, replica_groups=mesh['lat'=4,'lon'=8] {'lon'}, dimensions={0}, use_global_device_ids=true | all-gather | bytes 92160 | tf_op jit(solution)/shard_map/all_gather | solution.py:234
  33.5 0.1 reshape.81
  33.6 1.1 %dynamic-slice_bitcast_fusion.8 = (f32[20]{0:T(128)S(1)}, f32[20]{0:T(128)S(1)}, f32[20]{0:T(128)S(1)}, f32[20]{0:T(128)S(1)}, f32[20]{0:T(128)S(1)}, /*index=5*...) fusion(f32[9,640]{1,0:T(8,128)} %param.13, s32[]{:T(128)S(6)} %select_n.4, s32[]{:T(128)S(6)} %add.74, ...), kind=kLoop, calls=%fused_computation.103 | loop fusion | bytes 1476 | tf_op jit(solution)/shard_map/mul | solution.py:116
  34.7 0.2 reshape.83
  34.8 0.3 copy.76
  35.2 0.2 reshape.73
  35.4 3.2 %convolution_bitcast_fusion = f32[20,1056]{1,0:T(8,128)S(1)} fusion(bf16[2048,1056]{1,0:T(8,128)(2,1)} %bitcast.124, bf16[20,2048]{1,0:T(8,128)(2,1)S(1)} %reshape.73), kind=kOutput, calls=%fused_computation.3 | convolution fusion | flops 86507520 | bytes 4491776 | tf_op jit(solution)/shard_map/dot_general | solution.py:240
  38.6 0.4 fusion
  39.0 0.1 copy-done.1
  39.1 1.3 %fusion.1 = f32[20,2048]{1,0:T(8,128)S(1)} fusion(bf16[20,1056]{1,0:T(8,128)(2,1)S(1)} %fusion, bf16[2048,1056]{1,0:T(8,128)(2,1)S(1)} %bitcast.125), kind=kOutput, calls=%fused_computation.6 | convolution fusion | flops 86589440 | bytes 4531456 | tf_op jit(solution)/shard_map/dot_general | solution.py:244
  40.4 0.4 copy.81
  40.8 1.1 %copy.82 = f32[20,4,8,8,8]{0,4,3,2,1:T(8,128)} copy(f32[20,4,8,8,8]{0,4,2,3,1:T(8,128)S(1)} %bitcast.126) | data formatting | bytes 327680 | tf_op jit(solution)/shard_map/convert_element_type | solution.py:135
  41.9 1.7 %copy.83 = f32[20,32,64]{2,1,0:T(8,128)S(1)} copy(f32[20,32,64]{0,2,1:T(8,128)} %bitcast.127) | data formatting | bytes 327680 | tf_op jit(solution)/shard_map/convert_element_type | solution.py:135
  43.6 0.1 copy.77
  43.8 0.4 copy.78
  44.1 0.2 pad_slice_fusion.9
  44.4 1.1 %fusion.6 = bf16[20,32,64]{2,1,0:T(8,128)(2,1)S(1)} fusion(f32[20,32,64]{2,1,0:T(8,128)S(1)} %copy.83, bf16[20,32,64]{2,1,0:T(8,128)(2,1)S(1)} %copy.78, bf16[20,34,64]{2,1,0:T(8,128)(2,1)S(1)} %pad.4, bf16[20,34,1]{2,1,0:T(8,128)(2,1)S(1)} %get-tuple-element.6, bf16[20,34,1]{2,1,0:T(8,128)(2,1)S(1)} %get-tuple-element.5, f32[20]{0:T(128)S(1)} %get-tuple-element.15, ...), kind=kLoop, calls=%fused_computation.16 | loop fusion | flops 2007040 | bytes 1520128 | tf_op jit(solution)/shard_map/convert_element_type | solution.py:136
  45.5 0.4 copy.85
  45.9 0.1 copy.86
  46.0 0.3 copy.87
  46.3 0.1 reshape.84
  46.5 12.9 %all_to_all.10 = bf16[32,2,640]{2,1,0:T(2,128)(2,1)S(1)} all-to-all(bf16[32,2,640]{2,1,0:T(2,128)(2,1)S(1)} %reshape.84), channel_id=1, replica_groups=mesh['lat'=4,'lon'=8] {'lat','lon'}, dimensions={0} | all-to-all | bytes 163840 | tf_op jit(solution)/shard_map/all_to_all | solution.py:257
  59.3 0.2 reshape.85
  59.6 0.1 multiply_reduce_fusion
  59.7 0.1 copy.88
  59.9 3.6 %fusion.4 = bf16[640,8,8]{0,2,1:T(8,128)(2,1)} fusion(f32[640,64]{0,1:T(8,128)S(1)} %copy.88, bf16[1280,640]{1,0:T(8,128)(2,1)S(1)} %copy-done, bf16[640,1280]{1,0:T(8,128)(2,1)} %param.15, f32[640,64]{1,0:T(8,128)S(1)} %reshape.78, f32[640]{0:T(1024)S(1)} %copy-done.6, f32[64]{0:T(128)S(1)} %add_rsqrt_fusion), kind=kOutput, calls=%fused_computation.10 | convolution fusion | flops 215244800 | bytes 3689216 | tf_op jit(solution)/shard_map/dot_general | solution.py:128
  (19 shorter events, 0.3 us)
Async XLA Ops:
  0.0 59.8 %copy-start = (bf16[1280,640]{1,0:T(8,128)(2,1)S(1)}, bf16[1280,640]{1,0:T(8,128)(2,1)}, u32[]{:S(2)}) copy-start(bf16[1280,640]{1,0:T(8,128)(2,1)} %param.16) | copy-start | bytes 4915204
  0.0 15.6 %copy-start.3 = (f32[4,8,1056]{2,1,0:T(8,128)S(1)}, f32[4,8,1056]{2,1,0:T(8,128)}, u32[]{:S(2)}) copy-start(f32[4,8,1056]{2,1,0:T(8,128)} %constant.103) | copy-start | bytes 405508
  0.0 15.6 %copy-start.2 = (f32[8,8,1056]{2,1,0:T(8,128)S(1)}, f32[8,8,1056]{2,1,0:T(8,128)}, u32[]{:S(2)}) copy-start(f32[8,8,1056]{2,1,0:T(8,128)} %constant.104) | copy-start | bytes 811012
  3.8 30.9 %all-to-all-start = ((bf16[32,2,640]{2,1,0:T(2,128)(2,1)}), bf16[32,2,640]{2,1,0:T(2,128)(2,1)S(1)}, u32[]{:S(2)}, u32[]{:S(2)}) async-start(bf16[32,2,640]{2,1,0:T(2,128)(2,1)} %reshape.82), calls=%async_computation | async-start | bytes 163840 | tf_op jit(solution)/shard_map/all_to_all | solution.py:228
  11.1 7.9 %copy-start.5 = (f32[80,32]{0,1:T(8,128)S(1)}, f32[80,32]{0,1:T(8,128)}, u32[]{:S(2)}) copy-start(f32[80,32]{0,1:T(8,128)} %param.12) | copy-start | bytes 30724
  19.0 19.6 %copy-start.4 = (f32[32,1056]{1,0:T(8,128)S(1)}, f32[32,1056]{1,0:T(8,128)}, u32[]{:S(2)}) copy-start(f32[32,1056]{1,0:T(8,128)} %constant.98.clone) | copy-start | bytes 405508
  35.4 3.8 %copy-start.1 = (bf16[4,8,8,8,1056]{4,3,2,1,0:T(8,128)(2,1)S(1)}, bf16[4,8,8,8,1056]{4,3,2,1,0:T(8,128)(2,1)}, u32[]{:S(2)}) copy-start(bf16[4,8,8,8,1056]{4,3,2,1,0:T(8,128)(2,1)} %multiply_convert_fusion) | copy-start | bytes 12976132
  41.9 17.9 %copy-start.6 = (f32[640]{0:T(1024)S(1)}, f32[640]{0:T(1024)}, u32[]{:S(2)}) copy-start(f32[640]{0:T(1024)} %param.14) | copy-start | bytes 7684

commit v2 on v0

--- a/solution.py
+++ b/solution.py
@@ -1,8 +1,12 @@
+import functools
 import math
 
 import jax
 import jax.numpy as jnp
+import numpy as np
 from jax import lax
+from jax.experimental import pallas as pl
+from jax.experimental.pallas import tpu as pltpu
 from jax.sharding import PartitionSpec as P
 
 highest = lax.Precision.HIGHEST
@@ -88,7 +92,7 @@
         )
 
     degrees = jnp.arange(lat_count, dtype=jnp.int32)
-    unused, legendre = lax.scan(advance, (blank_rows, blank_rows, blank_rows), degrees, unroll=True)
+    unused, legendre = lax.scan(advance, (blank_rows, blank_rows, blank_rows), degrees)
     return legendre
 
 
@@ -169,9 +173,142 @@
     return result.reshape(channels, lat_rows, lon_cols)
 
 
+def transform_table(lat_count, lon_count):
+    theta = (np.arange(lat_count) + 0.5) * (math.pi / lat_count)
+    x, s = np.cos(theta), np.sin(theta)
+    phi = 2.0 * math.pi * np.arange(lon_count) / lon_count
+    columns, degree, weight = [], [], []
+    for m in range(lat_count):
+        k = np.arange(1, m + 1)
+        log_start = 0.5 * (
+            np.log((2 * m + 1) / (4 * math.pi)) + np.sum(np.log((2 * k - 1) / (2 * k)))
+        )
+        before, current = np.zeros(lat_count), np.exp(log_start + m * np.log(s))
+        for l in range(m, lat_count):
+            if l > m:
+                a = math.sqrt((4.0 * l * l - 1) / (l * l - m * m))
+                b = math.sqrt(((l - 1.0) ** 2 - m * m) / (4.0 * (l - 1) ** 2 - 1))
+                before, current = current, a * (x * current - b * before)
+            for wave in [np.cos(m * phi), -np.sin(m * phi)][: 1 if m == 0 else 2]:
+                columns.append((current[:, None] * wave[None, :]).reshape(-1))
+                degree.append(l)
+                weight.append(1.0 if m == 0 else 2.0)
+    select = np.arange(lat_count)[:, None] == np.array(degree)[None, :]
+    scaled = select * (np.array(weight) * (2.0 * math.pi / lon_count))[None, :]
+    quad = np.repeat(s * (math.pi / lat_count), lon_count)
+    return np.stack(columns, 1), scaled.astype(np.float32), quad.astype(np.float32)
+
+
+def exchange_kernel(lat_devices, devices, src_ref, dst_ref, send_sem, recv_sem, local_sem):
+    me = lax.axis_index("lon") * lat_devices + lax.axis_index("lat")
+
+    def place(index):
+        return (lax.rem(index, lat_devices), lax.div(index, lat_devices))
+
+    barrier = pltpu.get_barrier_semaphore()
+
+    def greet(step, carry):
+        peer = lax.rem(me + step, devices)
+        pl.semaphore_signal(
+            barrier, inc=1, device_id=place(peer), device_id_type=pl.DeviceIdType.MESH
+        )
+        return carry
+
+    lax.fori_loop(1, devices, greet, 0)
+    kept = pltpu.make_async_copy(src_ref.at[me], dst_ref.at[me], local_sem)
+    kept.start()
+    pl.semaphore_wait(barrier, devices - 1)
+
+    def copy(step, block, slot):
+        return pltpu.make_async_remote_copy(
+            src_ref=src_ref.at[block],
+            dst_ref=dst_ref.at[slot],
+            send_sem=send_sem.at[step],
+            recv_sem=recv_sem.at[step],
+            device_id=place(block),
+            device_id_type=pl.DeviceIdType.MESH,
+        )
+
+    def send(step, carry):
+        copy(step, lax.rem(me + step, devices), me).start()
+        return carry
+
+    def finish(step, carry):
+        copy(step, lax.rem(me + step, devices), me).wait_send()
+        source = lax.rem(me + devices - step, devices)
+        copy(step, source, source).wait_recv()
+        return carry
+
+    lax.fori_loop(1, devices, send, 0)
+    kept.wait()
+    lax.fori_loop(1, devices, finish, 0)
+
+
+def exchange(blocks, lat_devices, number):
+    devices = blocks.shape[0]
+    return pl.pallas_call(
+        functools.partial(exchange_kernel, lat_devices, devices),
+        out_shape=jax.ShapeDtypeStruct(blocks.shape, blocks.dtype),
+        in_specs=[pl.BlockSpec(memory_space=pltpu.VMEM)],
+        out_specs=pl.BlockSpec(memory_space=pltpu.VMEM),
+        scratch_shapes=[
+            pltpu.SemaphoreType.DMA((devices,)),
+            pltpu.SemaphoreType.DMA((devices,)),
+            pltpu.SemaphoreType.DMA,
+        ],
+        compiler_params=pltpu.CompilerParams(collective_id=number, has_side_effects=True),
+        name=f"exchange_{number}",
+    )(blocks)
+
+
+def whole_sphere(lat_devices, lon_devices, latent_field, spectral_filter, conv_weight, norm_gain, weight_in, weight_out):
+    channels, lat_rows, lon_cols = latent_field.shape
+    devices = lat_devices * lon_devices
+    lat_count, lon_count = lat_rows * lat_devices, lon_cols * lon_devices
+    points = lat_rows * lon_cols
+    own = channels // devices
+    me_lat, me_lon = lax.axis_index("lat"), lax.axis_index("lon")
+    packed = (devices, -1, math.gcd(own * points, 128))
+    table, select, quad = transform_table(lat_count, lon_count)
+    table = jnp.asarray(table.astype(jnp.bfloat16))
+    mine = exchange(latent_field.reshape(packed), lat_devices, 0)
+    own_filter = lax.dynamic_slice_in_dim(spectral_filter, me_lat * own, own, 0)
+    gain = lax.dot_general(
+        own_filter, jnp.asarray(select), (((1,), (0,)), ((), ())), precision=highest
+    )
+    grid = mine.reshape(lon_devices, lat_devices, own, lat_rows, lon_cols)
+    grid = jnp.transpose(grid, (2, 1, 3, 0, 4)).reshape(own, lat_count, lon_count)
+    flat = grid.reshape(own, lat_count * lon_count)
+    weighted = (flat.astype(jnp.float32) * jnp.asarray(quad)[None, :]).astype(jnp.bfloat16)
+    coefficients = lax.dot_general(
+        weighted, table, (((1,), (0,)), ((), ())), preferred_element_type=jnp.float32
+    )
+    coefficients = (coefficients * gain).astype(jnp.bfloat16)
+    spectral = lax.dot_general(
+        coefficients, table, (((1,), (1,)), ((), ())), preferred_element_type=jnp.float32
+    ).astype(jnp.bfloat16)
+    spectral = spectral.reshape(own, lat_count, lon_count)
+    start = (me_lon * lat_devices + me_lat) * own
+    own_kernel = lax.dynamic_slice_in_dim(conv_weight, start, own, 1)
+    rimmed = jnp.pad(grid, ((0, 0), (1, 1), (0, 0)))
+    mix = depthwise_core(wrap_columns(rimmed), own_kernel, lat_count, lon_count)
+    total = add_three(grid, spectral, mix)
+    total = total.reshape(own, lat_devices, lat_rows, lon_devices, lon_cols)
+    total = jnp.transpose(total, (3, 1, 0, 2, 4)).reshape(packed)
+    summed = exchange(total, lat_devices, 1)
+    result = channel_mlp(summed.reshape(channels, points), norm_gain, weight_in, weight_out)
+    return result.reshape(channels, lat_rows, lon_cols)
+
+
+def whole_or_banded(lat_devices, lon_devices, *arguments):
+    if arguments[0].shape[0] % (lat_devices * lon_devices) == 0:
+        return whole_sphere(lat_devices, lon_devices, *arguments)
+    return on_device(*arguments)
+
+
 def solution(mesh):
     return jax.shard_map(
-        on_device,
+        functools.partial(whole_or_banded, mesh.shape["lat"], mesh.shape["lon"]),
         mesh=mesh,
         in_specs=(P(None, "lat", "lon"), P("lon", None), P(), P(), P(), P()),
         out_specs=P(None, "lat", "lon"),

time: 106 us -> 50.5 us (0.48)
  other arithmetic: 25.6 us -> 1.59 us
  Pallas kernels: 0 us -> 22.7 us
  between operations: 21.1 us -> 0.17 us
  starting transfers between devices: 19.3 us -> 0 us
  blocking collectives: 11.5 us -> 0 us
  waiting for transfers between devices: 5.18 us -> 0 us
  matrix products: 5.57 us -> 10.3 us
    pallas_call x0 -> x2, Pallas kernels: none -> 22.7 us  [exchange(): pl.pallas_call(functools.partial(exchange_kernel, lat_devices, devices),...]
    or x16 -> x0, other arithmetic: 19.3 us -> none  [advance(): past_start | at_start]
    all_to_all x3 -> x0, starting transfers between devices: 14.1 us -> none  [the longest x1 6.35 us: on_device(): lax.all_to_all(latent_field, 'lon', split_axis=0, concat_axis=2, tiled=True)]
    all_to_all x1 -> x0, blocking collectives: 11.5 us -> none  [on_device(): lax.all_to_all(sector_sum, 'lon', split_axis=2, concat_axis=0, tiled=True)]
    reshape x1 -> x5, local copies, waits for them, and re-layouts: 2.97 us -> 8.79 us  [the longest x2 4.4 us: whole_sphere(): grid = mine.reshape(lon_devices, lat_devices, own, lat_rows, lon_cols)]
    ppermute x2 -> x0, starting transfers between devices: 5.21 us -> none  [the longest x1 3.92 us: with_halo(): lax.ppermute(tail, axis, [(i, (i + 1) % count) for i in range(ends)])]
    all_to_all x3 -> x0, waiting for transfers between devices: 5.18 us -> none  [the longest x1 4.37 us: on_device(): lax.all_to_all(synthesized, 'lat', split_axis=3, concat_axis=1, tiled=True)]
    dot_general x4 -> x3, matrix products: 2.21 us -> 6.64 us  [the longest x1 3.38 us: whole_sphere(): lax.dot_general(coefficients, table, (((1,), (1,)), ((), ())), preferred_...]
  transfers between devices with their start and end apart: 5 -> 0, of which waited for: 2 -> 0; matrix products, arithmetic and copies ran while one was open for 29% -> 0% of each run, Pallas kernels for 0% -> 0%
where the time goes in v2:
time: 50.5 us; the launch traced here: 50.2 us
  Pallas kernels  22.7 us (45%)
  local copies, waits for them, and re-layouts  15.5 us (31%)
  matrix products  10.3 us (20%)
  other arithmetic  1.59 us (3%)
    pallas_call x2, Pallas kernels, exchange(): pl.pallas_call(functools.partial(exchange_kernel, lat_devices, devices),...  22.7 us
    reshape x2, local copies, waits for them, and re-layouts, whole_sphere(): grid = mine.reshape(lon_devices, lat_devices, own, lat_rows, lon_cols)  4.4 us
    dot_general x1, matrix products, channel_mlp(): lax.dot_general(weight_out, hidden, (((0,), (0,)), ((), ())), preferred_e...  3.62 us
    dot_general x1, matrix products, whole_sphere(): lax.dot_general(coefficients, table, (((1,), (1,)), ((), ())), preferred_...  3.38 us
    dot_general x1, matrix products, whole_sphere(): lax.dot_general(weighted, table, (((1,), (0,)), ((), ())), preferred_elem...  2.9 us
    reshape x1, local copies, waits for them, and re-layouts, whole_sphere(): mine = exchange(latent_field.reshape(packed), lat_devices, 0)  2.01 us
    reshape x1, local copies, waits for them, and re-layouts, whole_sphere(): total = jnp.transpose(total, (3, 1, 0, 2, 4)).reshape(packed)  2.01 us
    unnamed x11, local copies, waits for them, and re-layouts  1.86 us

profile of v2, /device:TPU:0, one launch (start us, length us, event | category | flops | bytes accessed | tf_op | source)
XLA Modules:
  0.0 50.2 jit_solution(10355511643679724409)
XLA Ops:
  0.0 0.0 copy-start
  0.0 1.8 %copy.40 = bf16[640,8,8]{2,1,0:T(8,128)(2,1)S(1)} copy(bf16[640,8,8]{0,2,1:T(8,128)(2,1)} %param.9) | data formatting | bytes 163840 | tf_op args[0]
  1.8 2.0 %reshape.45.src_ref = bf16[32,10,128]{2,1,0:T(8,128)(2,1)} reshape(bf16[640,8,8]{2,1,0:T(8,128)(2,1)S(1)} %copy.40) | data formatting | bytes 163840 | tf_op jit(solution)/shard_map/reshape | solution.py:274
  3.9 11.8 %exchange_0.1 = bf16[32,10,128]{2,1,0:T(8,128)(2,1)} custom-call(bf16[32,10,128]{2,1,0:T(8,128)(2,1)} %reshape.45.src_ref), custom_call_target="tpu_custom_call" | custom-call | tf_op jit(solution)/shard_map/exchange_0/pallas_call | solution.py:249
  15.7 0.0 copy-start.3
  15.7 2.5 %reshape.46 = bf16[8,4,20,8,8]{4,3,2,1,0:T(8,128)(2,1)S(1)} reshape(bf16[32,10,128]{2,1,0:T(8,128)(2,1)} %exchange_0.1) | data formatting | bytes 163840 | tf_op jit(solution)/shard_map/reshape | solution.py:279
  18.2 1.9 %copy.41 = bf16[8,4,20,8,8]{2,4,0,3,1:T(8,128)(2,1)S(1)} copy(bf16[8,4,20,8,8]{4,3,2,1,0:T(8,128)(2,1)S(1)} %reshape.46) | data formatting | bytes 163840 | tf_op jit(solution)/shard_map/reshape | solution.py:279
  20.1 0.0 copy-done.3
  20.1 0.3 fusion.5
  20.4 0.0 copy-start.1
  20.4 0.0 copy-start.2
  20.5 2.9 %fusion.104 = f32[20,1024]{1,0:T(8,128)S(1)} fusion(bf16[20,2048]{0,1:T(8,128)(2,1)S(1)} %fusion.5, bf16[2048,1024]{1,0:T(8,128)(2,1)} %constant.92.clone), kind=kOutput, calls=%fused_computation.137 | convolution fusion | flops 83886080 | bytes 4358144 | tf_op jit(solution)/shard_map/dot_general | solution.py:283
  23.4 0.0 copy-done.1
  23.4 0.0 copy-done.2
  23.4 0.4 fusion.4
  23.7 3.4 %fusion = f32[20,2048]{1,0:T(8,128)S(1)} fusion(bf16[20,1024]{1,0:T(8,128)(2,1)S(1)} %fusion.4, bf16[2048,1024]{1,0:T(8,128)(2,1)} %constant.92.clone), kind=kOutput, calls=%fused_computation.1 | convolution fusion | flops 83968000 | bytes 4399104 | tf_op jit(solution)/shard_map/dot_general | solution.py:287
  27.1 0.1 reshape.52
  27.3 0.4 copy.42
  27.6 0.1 pad.4
  27.7 0.2 pad_slice_fusion.9
  27.9 1.1 %dynamic-slice_bitcast_fusion.8 = (f32[20]{0:T(128)S(1)}, f32[20]{0:T(128)S(1)}, f32[20]{0:T(128)S(1)}, f32[20]{0:T(128)S(1)}, f32[20]{0:T(128)S(1)}, /*index=5*...) fusion(f32[9,640]{1,0:T(8,128)} %param.11, s32[]{:T(128)S(6)} %select_n.7, s32[]{:T(128)S(6)} %add.77, ...), kind=kLoop, calls=%fused_computation.102 | loop fusion | bytes 1476 | tf_op jit(solution)/shard_map/mul | solution.py:118
  29.0 1.1 %fusion.7 = bf16[20,32,64]{2,1,0:T(8,128)(2,1)S(1)} fusion(f32[20,32,64]{2,1,0:T(8,128)S(1)} %reshape.52, bf16[20,32,64]{2,1,0:T(8,128)(2,1)S(1)} %copy.42, bf16[20,34,64]{2,1,0:T(8,128)(2,1)S(1)} %pad.4, bf16[20,34,1]{2,1,0:T(8,128)(2,1)S(1)} %get-tuple-element.6, bf16[20,34,1]{2,1,0:T(8,128)(2,1)S(1)} %get-tuple-element.5, f32[20]{0:T(128)S(1)} %get-tuple-element.15, ...), kind=kLoop, calls=%fused_computation.14 | loop fusion | flops 2007040 | bytes 1520128 | tf_op jit(solution)/shard_map/convert_element_type | solution.py:138
  30.1 0.4 copy.44
  30.5 1.9 %copy.45 = bf16[8,4,20,8,8]{4,3,2,1,0:T(8,128)(2,1)S(1)} copy(bf16[8,4,20,8,8]{2,4,0,3,1:T(8,128)(2,1)S(1)} %bitcast.113) | data formatting | bytes 163840 | tf_op jit(solution)/shard_map/transpose | solution.py:297
  32.3 0.0 copy-start.4
  32.4 2.0 %reshape.49.src_ref = bf16[32,10,128]{2,1,0:T(8,128)(2,1)} reshape(bf16[8,4,20,8,8]{4,3,2,1,0:T(8,128)(2,1)S(1)} %copy.45) | data formatting | bytes 163840 | tf_op jit(solution)/shard_map/reshape | solution.py:297
  34.4 10.9 %exchange_1.1 = bf16[32,10,128]{2,1,0:T(8,128)(2,1)} custom-call(bf16[32,10,128]{2,1,0:T(8,128)(2,1)} %reshape.49.src_ref), custom_call_target="tpu_custom_call" | custom-call | tf_op jit(solution)/shard_map/exchange_1/pallas_call | solution.py:249
  45.2 1.0 %reshape.53 = f32[640,64]{1,0:T(8,128)S(1)} reshape(bf16[32,10,128]{2,1,0:T(8,128)(2,1)} %exchange_1.1) | data formatting | bytes 245760 | tf_op jit(solution)/shard_map/convert_element_type | solution.py:123
  46.3 0.1 copy.46
  46.4 0.1 multiply_reduce_fusion
  46.5 0.0 copy-done
  46.6 3.6 %fusion.3 = bf16[640,8,8]{0,2,1:T(8,128)(2,1)} fusion(f32[640,64]{0,1:T(8,128)S(1)} %copy.46, bf16[1280,640]{1,0:T(8,128)(2,1)S(1)} %copy-done, bf16[640,1280]{1,0:T(8,128)(2,1)} %param.13, f32[640,64]{1,0:T(8,128)S(1)} %reshape.53, f32[640]{0:T(1024)S(1)} %copy-done.4, f32[64]{0:T(128)S(1)} %add_rsqrt_fusion), kind=kOutput, calls=%fused_computation.6 | convolution fusion | flops 215244800 | bytes 3689216 | tf_op jit(solution)/shard_map/dot_general | solution.py:130
  (2 shorter events, 0.0 us)
Async XLA Ops:
  0.0 46.5 %copy-start = (bf16[1280,640]{1,0:T(8,128)(2,1)S(1)}, bf16[1280,640]{1,0:T(8,128)(2,1)}, u32[]{:S(2)}) copy-start(bf16[1280,640]{1,0:T(8,128)(2,1)} %param.14) | copy-start | bytes 4915204
  15.7 4.4 %copy-start.3 = (f32[2048]{0:T(1024)S(1)}, f32[2048]{0:T(1024)}, u32[]{:S(2)}) copy-start(f32[2048]{0:T(1024)} %constant.94.clone) | copy-start | bytes 24580
  20.4 2.9 %copy-start.1 = (f32[32,1024]{1,0:T(8,128)S(1)}, f32[32,1024]{1,0:T(8,128)}, u32[]{:S(2)}) copy-start(f32[32,1024]{1,0:T(8,128)} %constant.93.clone) | copy-start | bytes 393220
  20.4 2.9 %copy-start.2 = (f32[80,32]{0,1:T(8,128)S(1)}, f32[80,32]{0,1:T(8,128)}, u32[]{:S(2)}) copy-start(f32[80,32]{0,1:T(8,128)} %param.10) | copy-start | bytes 30724
  32.3 14.2 %copy-start.4 = (f32[640]{0:T(1024)S(1)}, f32[640]{0:T(1024)}, u32[]{:S(2)}) copy-start(f32[640]{0:T(1024)} %param.12) | copy-start | bytes 7684

commit v3 on v2

--- a/solution.py
+++ b/solution.py
@@ -173,7 +173,11 @@
     return result.reshape(channels, lat_rows, lon_cols)
 
 
-def transform_table(lat_count, lon_count):
+def arrival_order(grid, lon_devices):
+    return grid.reshape(grid.shape[0], lon_devices, -1).transpose(1, 0, 2).reshape(-1)
+
+
+def transform_table(lat_count, lon_count, lon_devices):
     theta = (np.arange(lat_count) + 0.5) * (math.pi / lat_count)
     x, s = np.cos(theta), np.sin(theta)
     phi = 2.0 * math.pi * np.arange(lon_count) / lon_count
@@ -190,12 +194,13 @@
                 b = math.sqrt(((l - 1.0) ** 2 - m * m) / (4.0 * (l - 1) ** 2 - 1))
                 before, current = current, a * (x * current - b * before)
             for wave in [np.cos(m * phi), -np.sin(m * phi)][: 1 if m == 0 else 2]:
-                columns.append((current[:, None] * wave[None, :]).reshape(-1))
+                columns.append(arrival_order(current[:, None] * wave[None, :], lon_devices))
                 degree.append(l)
                 weight.append(1.0 if m == 0 else 2.0)
     select = np.arange(lat_count)[:, None] == np.array(degree)[None, :]
     scaled = select * (np.array(weight) * (2.0 * math.pi / lon_count))[None, :]
-    quad = np.repeat(s * (math.pi / lat_count), lon_count)
+    quad = np.broadcast_to((s * (math.pi / lat_count))[:, None], (lat_count, lon_count))
+    quad = arrival_order(quad, lon_devices)
     return np.stack(columns, 1), scaled.astype(np.float32), quad.astype(np.float32)
 
 
@@ -261,41 +266,69 @@
     )(blocks)
 
 
+def sphere_kernel(lat_count, lon_cols, flat_ref, quad_ref, table_ref, gain_ref, taps_ref, out_ref):
+    count = flat_ref.shape[1]
+    low = flat_ref[...]
+    field = low.astype(jnp.float32)
+    weighted = (field * quad_ref[...]).astype(jnp.bfloat16)
+    table = table_ref[...]
+    coefficients = jnp.dot(weighted, table, preferred_element_type=jnp.float32)
+    coefficients = (coefficients * gain_ref[...]).astype(jnp.bfloat16)
+    spectral = lax.dot_general(
+        coefficients, table, (((1,), (1,)), ((), ())), preferred_element_type=jnp.float32
+    )
+    point = lax.broadcasted_iota(jnp.int32, field.shape, 1)
+    column = lax.rem(point, lon_cols)
+    row = lax.rem(lax.div(point, lon_cols), lat_count)
+    jump = lat_count * lon_cols - (lon_cols - 1)
+    west = jnp.where(column == 0, pltpu.roll(field, jump, 1), pltpu.roll(field, 1, 1))
+    east = jnp.where(
+        column == lon_cols - 1, pltpu.roll(field, count - jump, 1), pltpu.roll(field, count - 1, 1)
+    )
+    taps = taps_ref[...]
+
+    def mixed(shift):
+        return (
+            taps[:, 3 * shift : 3 * shift + 1] * west
+            + taps[:, 3 * shift + 1 : 3 * shift + 2] * field
+            + taps[:, 3 * shift + 2 : 3 * shift + 3] * east
+        )
+
+    north = jnp.where(row == 0, 0.0, pltpu.roll(mixed(0), lon_cols, 1))
+    south = jnp.where(row == lat_count - 1, 0.0, pltpu.roll(mixed(2), count - lon_cols, 1))
+    mix = (north + mixed(1) + south).astype(jnp.bfloat16).astype(jnp.float32)
+    spectral = spectral.astype(jnp.bfloat16).astype(jnp.float32)
+    out_ref[...] = (field + spectral + mix).astype(jnp.bfloat16)
+
+
 def whole_sphere(lat_devices, lon_devices, latent_field, spectral_filter, conv_weight, norm_gain, weight_in, weight_out):
     channels, lat_rows, lon_cols = latent_field.shape
     devices = lat_devices * lon_devices
     lat_count, lon_count = lat_rows * lat_devices, lon_cols * lon_devices
     points = lat_rows * lon_cols
     own = channels // devices
+    padding = ((0, -own % 16), (0, 0))
     me_lat, me_lon = lax.axis_index("lat"), lax.axis_index("lon")
     packed = (devices, -1, math.gcd(own * points, 128))
-    table, select, quad = transform_table(lat_count, lon_count)
+    table, select, quad = transform_table(lat_count, lon_count, lon_devices)
     table = jnp.asarray(table.astype(jnp.bfloat16))
-    mine = exchange(latent_field.reshape(packed), lat_devices, 0)
     own_filter = lax.dynamic_slice_in_dim(spectral_filter, me_lat * own, own, 0)
     gain = lax.dot_general(
         own_filter, jnp.asarray(select), (((1,), (0,)), ((), ())), precision=highest
     )
-    grid = mine.reshape(lon_devices, lat_devices, own, lat_rows, lon_cols)
-    grid = jnp.transpose(grid, (2, 1, 3, 0, 4)).reshape(own, lat_count, lon_count)
-    flat = grid.reshape(own, lat_count * lon_count)
-    weighted = (flat.astype(jnp.float32) * jnp.asarray(quad)[None, :]).astype(jnp.bfloat16)
-    coefficients = lax.dot_general(
-        weighted, table, (((1,), (0,)), ((), ())), preferred_element_type=jnp.float32
-    )
-    coefficients = (coefficients * gain).astype(jnp.bfloat16)
-    spectral = lax.dot_general(
-        coefficients, table, (((1,), (1,)), ((), ())), preferred_element_type=jnp.float32
-    ).astype(jnp.bfloat16)
-    spectral = spectral.reshape(own, lat_count, lon_count)
     start = (me_lon * lat_devices + me_lat) * own
-    own_kernel = lax.dynamic_slice_in_dim(conv_weight, start, own, 1)
-    rimmed = jnp.pad(grid, ((0, 0), (1, 1), (0, 0)))
-    mix = depthwise_core(wrap_columns(rimmed), own_kernel, lat_count, lon_count)
-    total = add_three(grid, spectral, mix)
-    total = total.reshape(own, lat_devices, lat_rows, lon_devices, lon_cols)
-    total = jnp.transpose(total, (3, 1, 0, 2, 4)).reshape(packed)
-    summed = exchange(total, lat_devices, 1)
+    taps = lax.dynamic_slice_in_dim(conv_weight, start, own, 1).T
+    mine = exchange(latent_field.reshape(packed), lat_devices, 0)
+    flat = jnp.transpose(mine.reshape(devices, own, points), (1, 0, 2)).reshape(own, -1)
+    total = pl.pallas_call(
+        functools.partial(sphere_kernel, lat_count, lon_cols),
+        out_shape=jax.ShapeDtypeStruct((own + padding[0][1], devices * points), jnp.bfloat16),
+        in_specs=[pl.BlockSpec(memory_space=pltpu.VMEM)] * 5,
+        out_specs=pl.BlockSpec(memory_space=pltpu.VMEM),
+        name="sphere",
+    )(jnp.pad(flat, padding), jnp.asarray(quad)[None, :], table, jnp.pad(gain, padding), jnp.pad(taps, padding))
+    total = jnp.transpose(total[:own].reshape(own, devices, points), (1, 0, 2))
+    summed = exchange(total.reshape(packed), lat_devices, 1)
     result = channel_mlp(summed.reshape(channels, points), norm_gain, weight_in, weight_out)
     return result.reshape(channels, lat_rows, lon_cols)
 

time: 50.5 us -> 43.3 us (0.86)
  matrix products: 10.3 us -> 3.98 us
  Pallas kernels: 22.7 us -> 27.8 us
  local copies, waits for them, and re-layouts: 15.5 us -> 11 us
  other arithmetic: 1.59 us -> 0.11 us
    dot_general x2 -> x0, matrix products: 6.28 us -> none  [the longest x1 3.38 us: whole_sphere(): lax.dot_general(coefficients, table, (((1,), (1,)), ((), ())), preferred_...]
    pallas_call x0 -> x1, Pallas kernels: none -> 5.1 us  [whole_sphere(): pl.pallas_call(functools.partial(sphere_kernel, lat_count, lon_cols), out...]
    reshape x4 -> x5, local copies, waits for them, and re-layouts: 6.77 us -> 2.26 us  [the longest x1 1.06 us: whole_sphere(): mine.reshape(devices, own, points)]
    pad x1 -> x3, local copies, waits for them, and re-layouts: 0.07 us -> 1.92 us  [the longest x1 0.66 us: whole_sphere(): jnp.pad(gain, padding)]
    transpose x1, local copies, waits for them, and re-layouts: 1.86 us -> 0.02 us  [whole_sphere(): jnp.transpose(mine.reshape(devices, own, points), (1, 0, 2))]
    convert_element_type x2 -> x0, other arithmetic: 1.48 us -> none  [the longest x1 1.14 us: add_three(): return total.astype(jnp.bfloat16)]
    mul x1 -> x0, local copies, waits for them, and re-layouts: 1.09 us -> none  [depthwise_core(): kernel[3 * row_shift + col_shift][:, None, None] * piece]
    dynamic_slice x0 -> x1, local copies, waits for them, and re-layouts: none -> 0.79 us  [whole_sphere(): taps = lax.dynamic_slice_in_dim(conv_weight, start, own, 1).T]
where the time goes in v3:
time: 43.3 us; the launch traced here: 43 us
  Pallas kernels  27.8 us (64%)
  local copies, waits for them, and re-layouts  11 us (25%)
  matrix products  3.98 us (9%)
    pallas_call x2, Pallas kernels, exchange(): pl.pallas_call(functools.partial(exchange_kernel, lat_devices, devices),...  22.7 us
    pallas_call x1, Pallas kernels, whole_sphere(): pl.pallas_call(functools.partial(sphere_kernel, lat_count, lon_cols), out...  5.1 us
    dot_general x1, matrix products, channel_mlp(): lax.dot_general(weight_out, hidden, (((0,), (0,)), ((), ())), preferred_e...  3.62 us
    reshape x1, local copies, waits for them, and re-layouts, whole_sphere(): mine = exchange(latent_field.reshape(packed), lat_devices, 0)  2 us
    unnamed x10, local copies, waits for them, and re-layouts  1.94 us
    convert_element_type x2, local copies, waits for them, and re-layouts, channel_mlp(): summed = summed_low.astype(jnp.float32)  1.18 us
    reshape x1, local copies, waits for them, and re-layouts, whole_sphere(): mine.reshape(devices, own, points)  1.06 us
    slice x1, local copies, waits for them, and re-layouts, whole_sphere(): total = jnp.transpose(total[:own].reshape(own, devices, points), (1, 0, 2))  0.91 us

profile of v3, /device:TPU:0, one launch (start us, length us, event | category | flops | bytes accessed | tf_op | source)
XLA Modules:
  0.0 43.0 jit_solution(15651938340765307357)
XLA Ops:
  0.0 0.0 copy-start
  0.0 1.8 %copy.15 = bf16[640,8,8]{2,1,0:T(8,128)(2,1)S(1)} copy(bf16[640,8,8]{0,2,1:T(8,128)(2,1)} %param.9) | data formatting | bytes 163840 | tf_op args[0]
  1.8 0.0 copy-start.1
  1.8 0.0 copy-start.2
  1.9 2.0 %reshape.30.src_ref = bf16[32,10,128]{2,1,0:T(8,128)(2,1)} reshape(bf16[640,8,8]{2,1,0:T(8,128)(2,1)S(1)} %copy.15) | data formatting | bytes 163840 | tf_op jit(solution)/shard_map/reshape | solution.py:321
  3.9 11.8 %exchange_0.1 = bf16[32,10,128]{2,1,0:T(8,128)(2,1)} custom-call(bf16[32,10,128]{2,1,0:T(8,128)(2,1)} %reshape.30.src_ref), custom_call_target="tpu_custom_call" | custom-call | tf_op jit(solution)/shard_map/exchange_0/pallas_call | solution.py:254
  15.7 1.1 %reshape.31 = bf16[32,20,64]{2,1,0:T(8,128)(2,1)S(1)} reshape(bf16[32,10,128]{2,1,0:T(8,128)(2,1)} %exchange_0.1) | data formatting | bytes 163840 | tf_op jit(solution)/shard_map/reshape | solution.py:322
  16.8 0.2 reshape.32
  16.9 0.6 %pad.12.flat_ref = bf16[32,2048]{1,0:T(8,128)(2,1)} pad(bf16[20,2048]{1,0:T(8,128)(2,1)S(1)} %reshape.32, bf16[]{:T(256)} %constant.43.clone.1), padding=0_12x0_0 | pad | bytes 212994 | tf_op jit(solution)/shard_map/jit(_pad)/pad | solution.py:329
  17.6 0.0 copy-done.1
  17.6 0.0 copy-done.2
  17.6 0.4 fusion.57
  18.0 0.7 %pad.13.gain_ref = f32[32,1024]{1,0:T(8,128)} pad(f32[20,1024]{1,0:T(8,128)S(1)} %fusion.57, f32[]{:T(128)} %constant.13.clone.1), padding=0_12x0_0 | pad | bytes 212996 | tf_op jit(solution)/shard_map/jit(_pad)/pad | solution.py:329
  18.6 0.8 %constant_dynamic-slice_fusion = f32[9,20]{1,0:T(8,128)S(1)} fusion(f32[9,640]{1,0:T(8,128)} %param.11, s32[]{:T(128)S(6)} %select_n.7), kind=kLoop, calls=%fused_computation.67 | loop fusion | bytes 1444 | tf_op jit(solution)/shard_map/dynamic_slice | solution.py:320
  19.4 0.1 copy.20
  19.5 0.6 %pad.14.taps_ref = f32[32,9]{1,0:T(8,128)} pad(f32[20,9]{1,0:T(8,128)S(1)} %bitcast.85, f32[]{:T(128)} %constant.13.clone.1), padding=0_12x0_0 | pad | bytes 1876 | tf_op jit(solution)/shard_map/jit(_pad)/pad | solution.py:329
  20.1 5.1 %sphere.1 = bf16[32,2048]{1,0:T(8,128)(2,1)} custom-call(bf16[32,2048]{1,0:T(8,128)(2,1)} %pad.12.flat_ref, f32[1,2048]{1,0:T(1,128)} %constant.102.quad_ref, bf16[2048,1024]{1,0:T(8,128)(2,1)} %constant.93.clone.table_ref, f32[32,1024]{1,0:T(8,128)} %pad.13.gain_ref, f32[32,9]{1,0:T(8,128)} %pad.14.taps_ref), custom_call_target="tpu_custom_call" | custom-call | tf_op jit(solution)/shard_map/sphere/pallas_call | solution.py:323
  25.2 0.0 copy-start.3
  25.2 0.9 %slice.4 = bf16[20,2048]{1,0:T(8,128)(2,1)S(1)} slice(bf16[32,2048]{1,0:T(8,128)(2,1)} %sphere.1), slice={[0:20], [0:2048]} | slice | bytes 163840 | tf_op jit(solution)/shard_map/slice | solution.py:330
  26.1 0.2 reshape.33
  26.3 0.1 copy.22
  26.4 0.8 %reshape.34.src_ref = bf16[32,10,128]{2,1,0:T(8,128)(2,1)} reshape(bf16[32,20,64]{2,1,0:T(8,128)(2,1)S(1)} %bitcast.84) | data formatting | bytes 163840 | tf_op jit(solution)/shard_map/reshape | solution.py:331
  27.2 10.9 %exchange_1.1 = bf16[32,10,128]{2,1,0:T(8,128)(2,1)} custom-call(bf16[32,10,128]{2,1,0:T(8,128)(2,1)} %reshape.34.src_ref), custom_call_target="tpu_custom_call" | custom-call | tf_op jit(solution)/shard_map/exchange_1/pallas_call | solution.py:254
  38.1 1.0 %reshape.36 = f32[640,64]{1,0:T(8,128)S(1)} reshape(bf16[32,10,128]{2,1,0:T(8,128)(2,1)} %exchange_1.1) | data formatting | bytes 245760 | tf_op jit(solution)/shard_map/convert_element_type | solution.py:123
  39.1 0.1 copy.19
  39.2 0.1 multiply_reduce_fusion
  39.4 0.0 copy-done
  39.4 0.0 copy-done.3
  39.4 3.6 %fusion.2 = bf16[640,8,8]{0,2,1:T(8,128)(2,1)} fusion(f32[640,64]{0,1:T(8,128)S(1)} %copy.19, bf16[1280,640]{1,0:T(8,128)(2,1)S(1)} %copy-done, bf16[640,1280]{1,0:T(8,128)(2,1)} %param.13, f32[640,64]{1,0:T(8,128)S(1)} %reshape.36, f32[640]{0:T(1024)S(1)} %copy-done.3, f32[64]{0:T(128)S(1)} %add_rsqrt_fusion), kind=kOutput, calls=%fused_computation.3 | convolution fusion | flops 215244800 | bytes 3689216 | tf_op jit(solution)/shard_map/dot_general | solution.py:130
  (2 shorter events, 0.0 us)
Async XLA Ops:
  0.0 39.4 %copy-start = (bf16[1280,640]{1,0:T(8,128)(2,1)S(1)}, bf16[1280,640]{1,0:T(8,128)(2,1)}, u32[]{:S(2)}) copy-start(bf16[1280,640]{1,0:T(8,128)(2,1)} %param.14) | copy-start | bytes 4915204
  1.8 15.8 %copy-start.1 = (f32[32,1024]{1,0:T(8,128)S(1)}, f32[32,1024]{1,0:T(8,128)}, u32[]{:S(2)}) copy-start(f32[32,1024]{1,0:T(8,128)} %constant.94.clone) | copy-start | bytes 393220
  1.8 15.7 %copy-start.2 = (f32[80,32]{0,1:T(8,128)S(1)}, f32[80,32]{0,1:T(8,128)}, u32[]{:S(2)}) copy-start(f32[80,32]{0,1:T(8,128)} %param.10) | copy-start | bytes 30724
  25.2 14.1 %copy-start.3 = (f32[640]{0:T(1024)S(1)}, f32[640]{0:T(1024)}, u32[]{:S(2)}) copy-start(f32[640]{0:T(1024)} %param.12) | copy-start | bytes 7684
